TPU v7x, 32 devices: a whole 2x2x4 slice. The times are simulated.
32 devices in a mesh: expert: 8 (over y, x, core), replica: 4 (over z).
Axes of the slice: x: 2, y: 2, z: 4, core: 2. Of those that a mesh axis runs over, the one named last changes fastest.
Arguments:
- tokens_in: bfloat16 [8192, 2048], P(('expert', 'replica')), may hold values from -6 to 6
- cotangents: bfloat16 [8192, 8192], P(('expert', 'replica')), may hold values from -0.1796875 to 0.1796875
- left_root: bfloat16 [8, 2048, 2048], P('expert'), may hold values from -2 to 6, as said below
- right_root: bfloat16 [8, 8, 1024, 1024], P('expert', 'replica'), may hold values from -2 to 6, as said below
Outputs:
- update: bfloat16 [8, 2048, 8192], P('expert', None, 'replica')
Inputs may be any that keep to these rules, and one draw needn't show every extreme that they name: `left_root`: each matrix is symmetric. `right_root`: each block is symmetric.
All inputs are finite; a program needn't handle non-finite values.
Results may differ from a plain program's by a relative error of at most 0.0058.
Values may be sent and summed in bfloat16 or wider, within the bound.
A program may use at most 192 MiB of HBM per device.

v0:
```python
import jax
import jax.numpy as jnp
from jax import lax
from jax.sharding import PartitionSpec as P


def body(tokens_in, cotangents, left_root, right_root):
    expert_count = lax.axis_size("expert")
    replica_count = lax.axis_size("replica")
    local_experts = left_root.shape[0]
    width = left_root.shape[1]
    block_count = right_root.shape[1]
    block_size = right_root.shape[2]
    columns = cotangents.shape[1] // replica_count
    slot_count = tokens_in.shape[0] // (expert_count * local_experts)
    shaped = cotangents.reshape(1, expert_count, local_experts, slot_count, replica_count, columns)
    routed = lax.all_to_all(
        lax.all_to_all(shaped, "expert", split_axis=1, concat_axis=1, tiled=True),
        "replica",
        split_axis=4,
        concat_axis=0,
        tiled=True,
    )
    routed = routed.reshape(replica_count, expert_count, local_experts, slot_count, columns)
    tokens = tokens_in.reshape(expert_count, local_experts, slot_count, width)
    grouped = lax.all_to_all(tokens, "expert", split_axis=0, concat_axis=0, tiled=True)
    gradient = jnp.einsum(
        "rnxsd,rnxsf->xdf",
        lax.all_gather(grouped[None], "replica", axis=0, tiled=True),
        routed,
        preferred_element_type=jnp.float32,
    )
    gradient = gradient.astype(jnp.bfloat16)
    blocks = gradient.reshape(local_experts, width, block_count, block_size)
    applied = jnp.einsum("xdbk,xbkj->xdbj", blocks, right_root, preferred_element_type=jnp.float32)
    applied = applied.astype(jnp.bfloat16).reshape(local_experts, width, columns)
    update = jnp.einsum("xde,xef->xdf", left_root, applied, preferred_element_type=jnp.float32)
    return update.astype(jnp.bfloat16)


def solution(mesh):
    in_specs = (
        P(("expert", "replica"), None),
        P(("expert", "replica"), None),
        P("expert", None, None),
        P("expert", "replica", None, None),
    )
    out_specs = P("expert", None, "replica")
    return jax.shard_map(body, mesh=mesh, in_specs=in_specs, out_specs=out_specs, check_vma=False)
```

profile of v0, /device:TPU:0, one launch (start us, length us, event | category | flops | bytes accessed | tf_op | source)
XLA Modules:
  0.0 275.7 jit_solution(12691857189009747764)
XLA Ops:
  6.5 5.2 %all-to-all-start = ((bf16[8,1,32,2048]{3,2,1,0:T(8,128)(2,1)}), bf16[8,1,32,2048]{3,2,1,0:T(8,128)(2,1)S(1)}, u32[]{:S(2)}, u32[]{:S(2)}) async-start(bf16[8,1,32,2048]{3,2,1,0:T(8,128)(2,1)} %bitcast.41), calls=%async_computation | async-start | bytes 2097152 | tf_op jit(solution)/shard_map/all_to_all | solution.py:26
  11.7 7.8 %reshape.40 = bf16[1,8,1,32,4,2048]{5,4,3,1,2,0:T(4,128)(2,1)} reshape(bf16[256,8192]{1,0:T(8,128)(2,1)} %param.5) | data formatting | bytes 8388608 | tf_op jit(solution)/shard_map/reshape | solution.py:16
  19.5 6.6 %copy.13 = bf16[1,8,1,32,4,2048]{5,3,4,2,0,1:T(8,128)(2,1)} copy(bf16[1,8,1,32,4,2048]{5,4,3,1,2,0:T(4,128)(2,1)} %reshape.40) | data formatting | bytes 8388608 | tf_op jit(solution)/shard_map/reshape | solution.py:16
  26.1 1.0 all-to-all-done
  27.1 0.0 copy-start
  27.1 4.6 %all-to-all-start.1 = ((bf16[1,8,1,32,4,2048]{5,3,4,2,0,1:T(8,128)(2,1)}), bf16[1,8,1,32,4,2048]{5,3,4,2,0,1:T(8,128)(2,1)}, u32[]{:S(2)}, u32[]{:S(2)}) async-start(bf16[1,8,1,32,4,2048]{5,3,4,2,0,1:T(8,128)(2,1)} %copy.13), calls=%async_computation.1 | async-start | bytes 8388608 | tf_op jit(solution)/shard_map/all_to_all | solution.py:18
  31.7 0.0 all-gather.3.cloned.1.call-start
  31.8 0.0 copy-done
  31.8 0.7 all-gather.3.cloned.1.call-update
  32.4 48.4 %all-to-all-done.1 = bf16[1,8,1,32,4,2048]{5,3,4,2,0,1:T(8,128)(2,1)} async-done(((bf16[1,8,1,32,4,2048]{5,3,4,2,0,1:T(8,128)(2,1)}), bf16[1,8,1,32,4,2048]{5,3,4,2,0,1:T(8,128)(2,1)}, u32[]{:S(2)}, u32[]{:S(2)}) %all-to-all-start.1) | async-done | bytes 4194336 | tf_op jit(solution)/shard_map/all_to_all | solution.py:18
  80.8 4.8 %copy.14 = bf16[1,8,1,32,4,2048]{5,3,1,2,0,4:T(8,128)(2,1)} copy(bf16[1,8,1,32,4,2048]{5,3,4,2,0,1:T(8,128)(2,1)} %all-to-all-done.1) | data formatting | bytes 8388608 | tf_op jit(solution)/shard_map/all_to_all | solution.py:18
  85.6 5.0 %all-to-all-start.2 = ((bf16[1,8,1,32,4,2048]{5,3,1,2,0,4:T(8,128)(2,1)}), bf16[1,8,1,32,4,2048]{5,3,1,2,0,4:T(8,128)(2,1)}, u32[]{:S(2)}, u32[]{:S(2)}) async-start(bf16[1,8,1,32,4,2048]{5,3,1,2,0,4:T(8,128)(2,1)} %copy.14), calls=%async_computation.2 | async-start | bytes 8388608 | tf_op jit(solution)/shard_map/all_to_all | solution.py:17
  90.6 61.0 %all-gather.3.cloned.1.call-done = bf16[32,1,32,2048]{3,2,1,0:T(8,128)(2,1)} async-done(((bf16[8,1,32,2048]{3,2,1,0:T(8,128)(2,1)}), bf16[32,1,32,2048]{3,2,1,0:T(8,128)(2,1)}) %all-gather.3.cloned.1.call-update) | async-done | bytes 4194320 | tf_op jit(solution)/shard_map/all_gather | solution.py:29
  151.6 54.4 %all-to-all-done.2 = bf16[1,8,1,32,4,2048]{5,3,1,2,0,4:T(8,128)(2,1)} async-done(((bf16[1,8,1,32,4,2048]{5,3,1,2,0,4:T(8,128)(2,1)}), bf16[1,8,1,32,4,2048]{5,3,1,2,0,4:T(8,128)(2,1)}, u32[]{:S(2)}, u32[]{:S(2)}) %all-to-all-start.2) | async-done | bytes 4194336 | tf_op jit(solution)/shard_map/all_to_all | solution.py:17
  205.9 0.0 slice-start
  205.9 14.1 %bitcast_convert_fusion = bf16[2048,2048]{0,1:T(8,128)(2,1)} fusion(bf16[1,8,1,32,4,2048]{5,3,1,2,0,4:T(8,128)(2,1)} %all-to-all-done.2, bf16[4,8,32,2048]{3,2,1,0:T(8,128)(2,1)} %bitcast.44), kind=kOutput, calls=%fused_computation | convolution fusion | flops 8594128896 | bytes 16777216 | tf_op jit(solution)/shard_map/rnxsd,rnxsf->xdf/dot_general | solution.py:27
  220.1 0.0 slice-start.1
  220.1 14.8 %convolution_convert_fusion = bf16[2,2048,1024]{1,2,0:T(8,128)(2,1)} fusion(bf16[2048,2,1024]{0,2,1:T(8,128)(2,1)} %bitcast.45, bf16[1,2,1024,1024]{3,2,1,0:T(8,128)(2,1)} %param.7), kind=kOutput, calls=%fused_computation.4 | convolution fusion | flops 8594128896 | bytes 20971520 | tf_op jit(solution)/shard_map/xdbk,xbkj->xdbj/dot_general | solution.py:35
  234.9 0.0 slice-done
  234.9 0.0 slice-done.1
  234.9 21.8 %convert_bitcast_fusion = bf16[1,2048,2048]{1,2,0:T(8,128)(2,1)} fusion(bf16[2048,2048]{0,1:T(8,128)(2,1)} %bitcast.46, bf16[1,2048,2048]{2,1,0:T(8,128)(2,1)S(1)} %bitcast.43), kind=kOutput, calls=%fused_computation.3 | convolution fusion | flops 17184063488 | bytes 25165824 | tf_op jit(solution)/shard_map/xde,xef->xdf/dot_general | solution.py:37
  256.7 12.2 %copy.19 = bf16[1,2048,2048]{2,1,0:T(8,128)(2,1)} copy(bf16[1,2048,2048]{1,2,0:T(8,128)(2,1)} %convert_bitcast_fusion) | data formatting | bytes 16777216 | tf_op jit(solution)/shard_map/convert_element_type | solution.py:38
  (1 shorter events, 0.0 us)
Async XLA Ops:
  6.5 20.6 %all-to-all-start = ((bf16[8,1,32,2048]{3,2,1,0:T(8,128)(2,1)}), bf16[8,1,32,2048]{3,2,1,0:T(8,128)(2,1)S(1)}, u32[]{:S(2)}, u32[]{:S(2)}) async-start(bf16[8,1,32,2048]{3,2,1,0:T(8,128)(2,1)} %bitcast.41), calls=%async_computation | async-start | bytes 2097152 | tf_op jit(solution)/shard_map/all_to_all | solution.py:26
  27.1 4.6 %copy-start = (bf16[8,1,32,2048]{3,2,1,0:T(8,128)(2,1)}, bf16[8,1,32,2048]{3,2,1,0:T(8,128)(2,1)S(1)}, u32[]{:S(2)}) copy-start(bf16[8,1,32,2048]{3,2,1,0:T(8,128)(2,1)S(1)} %all-to-all-done) | copy-start | bytes 3145732
  27.1 53.7 %all-to-all-start.1 = ((bf16[1,8,1,32,4,2048]{5,3,4,2,0,1:T(8,128)(2,1)}), bf16[1,8,1,32,4,2048]{5,3,4,2,0,1:T(8,128)(2,1)}, u32[]{:S(2)}, u32[]{:S(2)}) async-start(bf16[1,8,1,32,4,2048]{5,3,4,2,0,1:T(8,128)(2,1)} %copy.13), calls=%async_computation.1 | async-start | bytes 8388608 | tf_op jit(solution)/shard_map/all_to_all | solution.py:18
  31.7 119.9 %all-gather.3.cloned.1.call-start = ((), (), s32[]{:S(2)}) async-start(), calls=%async_computation.3 | async-start | bytes 5242880 | tf_op jit(solution)/shard_map/all_gather | solution.py:29
  85.6 120.3 %all-to-all-start.2 = ((bf16[1,8,1,32,4,2048]{5,3,1,2,0,4:T(8,128)(2,1)}), bf16[1,8,1,32,4,2048]{5,3,1,2,0,4:T(8,128)(2,1)}, u32[]{:S(2)}, u32[]{:S(2)}) async-start(bf16[1,8,1,32,4,2048]{5,3,1,2,0,4:T(8,128)(2,1)} %copy.14), calls=%async_computation.2 | async-start | bytes 8388608 | tf_op jit(solution)/shard_map/all_to_all | solution.py:17
  205.9 28.9 %slice-start = ((s8[8388608]{0:T(1024)(128)(4,1)}), s8[4194304]{0:T(1024)(128)(4,1)S(1)}, s32[]{:S(2)}) async-start(s8[8388608]{0:T(1024)(128)(4,1)} %bitcast.42), calls=%async_computation.4 | async-start | bytes 8388608
  220.1 14.8 %slice-start.1 = ((s8[8388608]{0:T(1024)(128)(4,1)}), s8[4194304]{0:T(1024)(128)(4,1)S(1)}, s32[]{:S(2)}) async-start(s8[8388608]{0:T(1024)(128)(4,1)} %bitcast.42), calls=%async_computation.5 | async-start | bytes 8388608
Sparse Core Ops, SparseCore 0:
  34.1 117.4 all-gather.2
where the time goes:
time: 277 us; the launch traced here: 276 us
  waiting for transfers between devices  165 us (60%)
  matrix products  50.7 us (18%)
  local copies, waits for them, and re-layouts  31.4 us (11%)
  starting transfers between devices  14.8 us (5%)
  between operations  13.4 us (5%)
    all_gather x1, waiting for transfers between devices, body(): lax.all_gather(grouped[None], 'replica', axis=0, tiled=True)  61 us
    all_to_all x1, waiting for transfers between devices, body(): lax.all_to_all(lax.all_to_all(shaped, 'expert', split_axis=1, concat_axis...  54.4 us
    all_to_all x1, waiting for transfers between devices, body(): lax.all_to_all(shaped, 'expert', split_axis=1, concat_axis=1, tiled=True)  48.4 us
    dot_general x1, matrix products, body(): jnp.einsum('xde,xef->xdf', left_root, applied, preferred_element_type=jnp...  21.8 us
    dot_general x1, matrix products, body(): jnp.einsum('xdbk,xbkj->xdbj', blocks, right_root, preferred_element_type=...  14.8 us
    reshape x2, local copies, waits for them, and re-layouts, body(): cotangents.reshape(1, expert_count, local_experts, slot_count, replica_co...  14.4 us
    dot_general x1, matrix products, body(): jnp.einsum('rnxsd,rnxsf->xdf', lax.all_gather(grouped[None], 'replica', a...  14.1 us
    convert_element_type x1, local copies, waits for them, and re-layouts, body(): return update.astype(jnp.bfloat16)  12.2 us
  transfers between devices with their start and end apart: 4, of which 4 were waited for; matrix products, arithmetic and copies ran while one was open for 7% of the time, Pallas kernels for 0%

commit v1 on v0

v1 whole, which is shorter than its diff:
```python
import functools
import jax
import jax.numpy as jnp
from jax import lax
from jax.experimental import pallas as pl
from jax.experimental.pallas import tpu as pltpu
from jax.sharding import PartitionSpec as P


def tile_of(size, most):
    return most if size % most == 0 else size


def route_kernel(
    ne, nr, tok_ref, cot_ref, left_ref, right_ref, x_ref, y_ref,
    tok, cot, left, right, x, y,
    plane_send, up_send, down_send, tok_recv, cot_send, cot_recv, local,
):
    e = lax.axis_index("expert")
    r = lax.axis_index("replica")
    rows = tok_ref.shape[0] // ne
    group = rows * ne
    width = tok.shape[1]
    cols = cot.shape[1]
    blocks, order = right_ref.shape[0], right_ref.shape[1]

    load_left = pltpu.make_async_copy(left_ref, left, local.at[0])
    load_right = pltpu.make_async_copy(right_ref, right, local.at[1])
    load_left.start()
    load_right.start()

    barrier = pltpu.get_barrier_semaphore()

    @pl.loop(1, ne * nr)
    def _(k):
        pl.semaphore_signal(
            barrier, inc=1,
            device_id={"expert": (e + k % ne) % ne, "replica": (r + k // ne) % nr},
        )

    pl.semaphore_wait(barrier, ne * nr - 1)

    def span(origin, source):
        return pl.ds(pl.multiple_of((origin * ne + source) * rows, rows), rows)

    def own_rows(target):
        return pl.ds(pl.multiple_of(target * rows, rows), rows)

    def own_cols(target):
        return pl.ds(pl.multiple_of(target * cols, cols), cols)

    def plane_copy(target):
        return pltpu.make_async_remote_copy(
            tok_ref.at[own_rows(target)], tok.at[span(r, e)],
            plane_send.at[target], tok_recv.at[r * ne + e],
            device_id={"expert": target, "replica": r},
        )

    def relay(origin, source, up):
        at = span(origin, source)
        k = origin * ne + source
        return pltpu.make_async_remote_copy(
            tok.at[at], tok.at[at],
            (up_send if up else down_send).at[k], tok_recv.at[k],
            device_id={"expert": e, "replica": r + 1 if up else r - 1},
        )

    def tok_wait(origin, source):
        pltpu.make_async_remote_copy(
            tok.at[span(origin, source)], tok.at[span(origin, source)],
            up_send.at[0], tok_recv.at[origin * ne + source],
            device_id={"expert": e, "replica": (r + 1) % nr},
        ).wait_recv()

    def cot_copy(te, tr):
        return pltpu.make_async_remote_copy(
            cot_ref.at[own_rows(te), own_cols(tr)], cot.at[span(r, e)],
            cot_send.at[tr * ne + te], cot_recv.at[r * ne + e],
            device_id={"expert": te, "replica": tr},
        )

    def send_cots(te, distance):
        for tr in (r + distance, r - distance):
            @pl.when((tr >= 0) & (tr < nr))
            def _():
                cot_copy(te, tr).start()

    def forward(origin, source, up):
        ahead = (r + 1 < nr) if up else (r > 0)

        @pl.when(ahead)
        def _():
            relay(origin, source, up).start()

    own_tok = pltpu.make_async_copy(tok_ref.at[own_rows(e)], tok.at[span(r, e)], local.at[2])
    own_cot = pltpu.make_async_copy(cot_ref.at[own_rows(e), own_cols(r)], cot.at[span(r, e)], local.at[3])
    own_tok.start()
    own_cot.start()

    @pl.loop(1, ne)
    def _(k):
        plane_copy((e + k) % ne).start()

    own_tok.wait()

    @pl.loop(0, ne)
    def _(k):
        source = (e + ne - k) % ne

        @pl.when(k > 0)
        def _():
            tok_wait(r, source)

        forward(r, source, True)
        forward(r, source, False)
        for distance in range(nr - 1, 1, -1):
            send_cots((e + k) % ne, distance)

    for distance in range(1, nr):
        @pl.loop(0, ne)
        def _(k):
            source = (e + ne - k) % ne

            @pl.when(r - distance >= 0)
            def _():
                tok_wait(r - distance, source)
                forward(r - distance, source, True)

            @pl.when(r + distance < nr)
            def _():
                tok_wait(r + distance, source)
                forward(r + distance, source, False)

            if distance == 1:
                send_cots((e + k) % ne, 1)

                @pl.when(k > 0)
                def _():
                    cot_copy((e + k) % ne, r).start()

    load_left.wait()
    step = tile_of(width, 256)

    @pl.loop(0, nr)
    def _(g):
        columns = pl.ds(pl.multiple_of(g * group, group), group)

        @pl.loop(0, width // step)
        def _(i):
            part = pl.ds(pl.multiple_of(i * step, step), step)
            x[part, columns] = lax.dot_general(
                left[part, :], tok[columns, :], (((1,), (1,)), ((), ())),
                preferred_element_type=jnp.float32,
            ).astype(x.dtype)

    store_x = pltpu.make_async_copy(x, x_ref, local.at[2])
    store_x.start()
    load_right.wait()
    own_cot.wait()

    def store_y(g):
        at = pl.ds(pl.multiple_of(g * group, group), group)
        return pltpu.make_async_copy(y.at[at], y_ref.at[at], local.at[4 + g])

    @pl.loop(0, nr)
    def _(i):
        g = (r + nr // 2 + i) % nr

        @pl.loop(0, ne)
        def _(s):
            @pl.when((s != e) | (g != r))
            def _():
                pltpu.make_async_remote_copy(
                    cot_ref.at[own_rows(s), own_cols(g)], cot.at[span(g, s)],
                    cot_send.at[0], cot_recv.at[g * ne + s],
                    device_id={"expert": (e + 1) % ne, "replica": r},
                ).wait_recv()

        at = pl.ds(pl.multiple_of(g * group, group), group)
        for b in range(blocks):
            inside = slice(b * order, (b + 1) * order)
            y[at, inside] = jnp.dot(
                cot[at, inside], right[b], preferred_element_type=jnp.float32
            ).astype(y.dtype)
        store_y(g).start()

    @pl.loop(1, ne)
    def _(k):
        plane_copy((e + k) % ne).wait_send()

    @pl.loop(0, ne * nr)
    def _(k):
        tr, te = k // ne, k % ne

        @pl.when((te != e) | (tr != r))
        def _():
            cot_copy(te, tr).wait_send()

        @pl.when((tr <= r) & (r + 1 < nr))
        def _():
            relay(tr, te, True).wait_send()

        @pl.when((tr >= r) & (r > 0))
        def _():
            relay(tr, te, False).wait_send()

    store_x.wait()

    @pl.loop(0, nr)
    def _(g):
        store_y(g).wait()


def body(tokens_in, cotangents, left_root, right_root):
    ne, nr = lax.axis_size("expert"), lax.axis_size("replica")
    assert left_root.shape[0] == 1
    width = tokens_in.shape[1]
    columns = cotangents.shape[1] // nr
    total = tokens_in.shape[0] * nr
    blocks, order = right_root.shape[1], right_root.shape[2]
    anywhere = pl.BlockSpec(memory_space=pl.ANY)
    n = ne * nr
    dtype = jnp.bfloat16
    dma = pltpu.SemaphoreType.DMA
    x, y = pl.pallas_call(
        functools.partial(route_kernel, ne, nr),
        out_shape=[
            jax.ShapeDtypeStruct((width, total), dtype),
            jax.ShapeDtypeStruct((total, columns), dtype),
        ],
        in_specs=[anywhere] * 4,
        out_specs=[anywhere] * 2,
        scratch_shapes=[
            pltpu.VMEM((total, width), dtype),
            pltpu.VMEM((total, columns), dtype),
            pltpu.VMEM((width, width), dtype),
            pltpu.VMEM((blocks, order, order), dtype),
            pltpu.VMEM((width, total), dtype),
            pltpu.VMEM((total, columns), dtype),
            dma((ne,)), dma((n,)), dma((n,)), dma((n,)), dma((n,)), dma((n,)), dma((4 + nr,)),
        ],
        compiler_params=pltpu.CompilerParams(collective_id=0, has_side_effects=True),
    )(tokens_in, cotangents, left_root[0], right_root[0])
    return jnp.dot(x, y, preferred_element_type=jnp.float32).astype(dtype)[None]


def solution(mesh):
    in_specs = (
        P(("expert", "replica"), None),
        P(("expert", "replica"), None),
        P("expert", None, None),
        P("expert", "replica", None, None),
    )
    out_specs = P("expert", None, "replica")
    return jax.shard_map(body, mesh=mesh, in_specs=in_specs, out_specs=out_specs, check_vma=False)
```

time: 277 us -> 183 us (0.66)
  Pallas kernels: 0 us -> 169 us
  waiting for transfers between devices: 165 us -> 0 us
  matrix products: 50.7 us -> 13.9 us
  local copies, waits for them, and re-layouts: 31.4 us -> 0 us
  starting transfers between devices: 14.8 us -> 0 us
  between operations: 13.4 us -> 0.01 us
    pallas_call x0 -> x1, Pallas kernels: none -> 169 us  [body(): pl.pallas_call(functools.partial(route_kernel, ne, nr), out_shape=[jax.Sh...]
    all_to_all x3 -> x0, waiting for transfers between devices: 104 us -> none  [the longest x1 54.4 us: body(): lax.all_to_all(lax.all_to_all(shaped, 'expert', split_axis=1, concat_axis...]
    all_gather x1 -> x0, waiting for transfers between devices: 61 us -> none  [body(): lax.all_gather(grouped[None], 'replica', axis=0, tiled=True)]
    dot_general x3 -> x1, matrix products: 50.7 us -> 13.9 us  [body(): return jnp.dot(x, y, preferred_element_type=jnp.float32).astype(dtype)[None]]
    all_to_all x3 -> x0, starting transfers between devices: 14.8 us -> none  [the longest x1 5.2 us: body(): lax.all_to_all(tokens, 'expert', split_axis=0, concat_axis=0, tiled=True)]
    reshape x2 -> x0, local copies, waits for them, and re-layouts: 14.4 us -> none  [body(): cotangents.reshape(1, expert_count, local_experts, slot_count, replica_co...]
    convert_element_type x1 -> x0, local copies, waits for them, and re-layouts: 12.2 us -> none  [body(): return update.astype(jnp.bfloat16)]
    all_to_all x1 -> x0, local copies, waits for them, and re-layouts: 4.79 us -> none  [body(): lax.all_to_all(shaped, 'expert', split_axis=1, concat_axis=1, tiled=True)]
  transfers between devices with their start and end apart: 4 -> 0, of which waited for: 4 -> 0; matrix products, arithmetic and copies ran while one was open for 7% -> 0% of each run, Pallas kernels for 0% -> 0%
where the time goes in v1:
time: 183 us
  Pallas kernels  169 us (92%)
  matrix products  13.9 us (8%)
    pallas_call x1, Pallas kernels, body(): pl.pallas_call(functools.partial(route_kernel, ne, nr), out_shape=[jax.Sh...  169 us
    dot_general x1, matrix products, body(): return jnp.dot(x, y, preferred_element_type=jnp.float32).astype(dtype)[None]  13.9 us

profile of v1, /device:TPU:0, one launch (start us, length us, event | category | flops | bytes accessed | tf_op | source)
XLA Modules:
  0.0 183.2 jit_solution(6983009556052265822)
XLA Ops:
  0.0 169.3 %shard_map.46 = (bf16[2048,1024]{1,0:T(8,128)(2,1)}, bf16[1024,2048]{1,0:T(8,128)(2,1)}) custom-call(bf16[256,2048]{1,0:T(8,128)(2,1)} %tok_ref.1, bf16[256,8192]{1,0:T(8,128)(2,1)} %cot_ref.1, bf16[2048,2048]{1,0:T(8,128)(2,1)} %bitcast.6, bf16[2,1024,1024]{2,1,0:T(8,128)(2,1)} %bitcast.7), custom_call_target="tpu_custom_call" | custom-call | tf_op jit(solution)/shard_map/pallas_call | solution.py:225
  169.3 13.9 %convert_bitcast_fusion = bf16[1,2048,2048]{2,1,0:T(8,128)(2,1)} fusion(bf16[2048,1024]{1,0:T(8,128)(2,1)} %get-tuple-element.7, bf16[1024,2048]{1,0:T(8,128)(2,1)} %get-tuple-element.8), kind=kOutput, calls=%fused_computation | convolution fusion | flops 8594128896 | bytes 16777216 | tf_op jit(solution)/shard_map/dot_general | solution.py:244

commit v2 on v1

--- a/solution.py
+++ b/solution.py
@@ -116,33 +116,9 @@
         for distance in range(nr - 1, 1, -1):
             send_cots((e + k) % ne, distance)
 
-    for distance in range(1, nr):
-        @pl.loop(0, ne)
-        def _(k):
-            source = (e + ne - k) % ne
-
-            @pl.when(r - distance >= 0)
-            def _():
-                tok_wait(r - distance, source)
-                forward(r - distance, source, True)
-
-            @pl.when(r + distance < nr)
-            def _():
-                tok_wait(r + distance, source)
-                forward(r + distance, source, False)
-
-            if distance == 1:
-                send_cots((e + k) % ne, 1)
-
-                @pl.when(k > 0)
-                def _():
-                    cot_copy((e + k) % ne, r).start()
-
-    load_left.wait()
     step = tile_of(width, 256)
 
-    @pl.loop(0, nr)
-    def _(g):
+    def make_x(g):
         columns = pl.ds(pl.multiple_of(g * group, group), group)
 
         @pl.loop(0, width // step)
@@ -152,6 +128,36 @@
                 left[part, :], tok[columns, :], (((1,), (1,)), ((), ())),
                 preferred_element_type=jnp.float32,
             ).astype(x.dtype)
+
+    for distance in range(1, nr):
+        @pl.loop(0, ne)
+        def _(k):
+            source = (e + ne - k) % ne
+
+            @pl.when(r - distance >= 0)
+            def _():
+                tok_wait(r - distance, source)
+                forward(r - distance, source, True)
+
+            @pl.when(r + distance < nr)
+            def _():
+                tok_wait(r + distance, source)
+                forward(r + distance, source, False)
+
+            if distance == 1:
+                send_cots((e + k) % ne, 1)
+
+                @pl.when(k > 0)
+                def _():
+                    cot_copy((e + k) % ne, r).start()
+
+        if distance == 1:
+            load_left.wait()
+            make_x(r)
+        for g in (r - distance, r + distance):
+            @pl.when((g >= 0) & (g < nr))
+            def _():
+                make_x(g)
 
     store_x = pltpu.make_async_copy(x, x_ref, local.at[2])
     store_x.start()

time: 183 us -> 172 us (0.940)
  Pallas kernels: 169 us -> 158 us
    pallas_call x1, Pallas kernels: 169 us -> 158 us  [body(): pl.pallas_call(functools.partial(route_kernel, ne, nr), out_shape=[jax.Sh...]
where the time goes in v2:
time: 172 us
  Pallas kernels  158 us (92%)
  matrix products  13.9 us (8%)
    pallas_call x1, Pallas kernels, body(): pl.pallas_call(functools.partial(route_kernel, ne, nr), out_shape=[jax.Sh...  158 us
    dot_general x1, matrix products, body(): return jnp.dot(x, y, preferred_element_type=jnp.float32).astype(dtype)[None]  13.9 us

profile of v2, /device:TPU:0, one launch (start us, length us, event | category | flops | bytes accessed | tf_op | source)
XLA Modules:
  0.0 171.9 jit_solution(7608650627281876234)
XLA Ops:
  0.0 158.0 %shard_map.46 = (bf16[2048,1024]{1,0:T(8,128)(2,1)}, bf16[1024,2048]{1,0:T(8,128)(2,1)}) custom-call(bf16[256,2048]{1,0:T(8,128)(2,1)} %tok_ref.1, bf16[256,8192]{1,0:T(8,128)(2,1)} %cot_ref.1, bf16[2048,2048]{1,0:T(8,128)(2,1)} %bitcast.6, bf16[2,1024,1024]{2,1,0:T(8,128)(2,1)} %bitcast.7), custom_call_target="tpu_custom_call" | custom-call | tf_op jit(solution)/shard_map/pallas_call | solution.py:231
  158.0 13.9 %convert_bitcast_fusion = bf16[1,2048,2048]{2,1,0:T(8,128)(2,1)} fusion(bf16[2048,1024]{1,0:T(8,128)(2,1)} %get-tuple-element.7, bf16[1024,2048]{1,0:T(8,128)(2,1)} %get-tuple-element.8), kind=kOutput, calls=%fused_computation | convolution fusion | flops 8594128896 | bytes 16777216 | tf_op jit(solution)/shard_map/dot_general | solution.py:250
